TPU v7x, 32 devices: a whole 2x2x4 slice. The times are simulated.
32 devices in a mesh: tm: 16 (over z, y, core), chan: 2 (over x).
Axes of the slice: x: 2, y: 2, z: 4, core: 2. Of those that a mesh axis runs over, the one named last changes fastest.
Arguments:
- signal: bfloat16 [32768, 512], P('tm', 'chan'), may hold values from -72 to 72
- tapers: bfloat16 [8, 4096], replicated, may hold values from -0.09375 to 0.09375
- eigenvalues: float32 [8], replicated, may hold values from 0.05 to 1
Outputs:
- relative_psd: float32 [2048, 512], P('tm', 'chan')
All inputs are finite; a program needn't handle non-finite values.
Results may differ from a plain program's by a relative error of at most 0.0026.
The roundings to bfloat16 on the way count: a program that leaves them out, or rounds other values in their place, can miss the bound.
Values may be sent and summed in bfloat16 or wider, within the bound.
No kernel may reach another device: no remote copies, remote signals or barrier semaphores. Data moves between devices by JAX's collectives and lax.ppermute only.
A program may use at most 64 MiB of HBM per device.

v0:
```python
import math

import jax
import jax.numpy as jnp
from jax import lax
from jax.sharding import PartitionSpec as P

P_SIZE = 32
Q = 128


EPSILON = 1e-06


def dft_tables(outer_size, inner_size):
    inner = jnp.arange(inner_size, dtype=jnp.int32)
    outer = jnp.arange(outer_size, dtype=jnp.int32)
    halves = jnp.arange(outer_size // 2, dtype=jnp.int32)
    angle_first = (inner[:, None] * inner[None, :] % inner_size).astype(jnp.float32) * (
        2.0 * math.pi / inner_size
    )
    first_table = jnp.concatenate([jnp.cos(angle_first), -jnp.sin(angle_first)], axis=0).astype(
        jnp.bfloat16
    )
    angle_twist = (inner[:, None] * outer[None, :] % (outer_size * inner_size)).astype(
        jnp.float32
    ) * (2.0 * math.pi / (outer_size * inner_size))
    twist_cos = jnp.cos(angle_twist)[:, :, None, None]
    twist_sin = jnp.sin(angle_twist)[:, :, None, None]
    angle_last = (outer[:, None] * halves[None, :] % outer_size).astype(jnp.float32) * (
        2.0 * math.pi / outer_size
    )
    last_cos = jnp.cos(angle_last).astype(jnp.bfloat16)
    last_sin = jnp.sin(angle_last).astype(jnp.bfloat16)
    return (first_table, twist_cos, twist_sin, last_cos, last_sin)


def taper_power(tapered, tables):
    first_table, twist_cos, twist_sin, last_cos, last_sin = tables
    inner_size = tapered.shape[0]
    first = jnp.einsum("jn,npsc->jpsc", first_table, tapered, preferred_element_type=jnp.float32)
    first_real = first[:inner_size]
    first_imaginary = first[inner_size:]
    twist_real = (first_real * twist_cos + first_imaginary * twist_sin).astype(jnp.bfloat16)
    twist_imaginary = (first_imaginary * twist_cos - first_real * twist_sin).astype(jnp.bfloat16)
    last_real = jnp.einsum(
        "pa,kpsc->aksc", last_cos, twist_real, preferred_element_type=jnp.float32
    ) + jnp.einsum("pa,kpsc->aksc", last_sin, twist_imaginary, preferred_element_type=jnp.float32)
    last_imaginary = jnp.einsum(
        "pa,kpsc->aksc", last_cos, twist_imaginary, preferred_element_type=jnp.float32
    ) - jnp.einsum("pa,kpsc->aksc", last_sin, twist_real, preferred_element_type=jnp.float32)
    return last_real * last_real + last_imaginary * last_imaginary


def local(signal, tapers, eigenvalues):
    row_count, chan_count = signal.shape
    outer_size = P_SIZE
    inner_size = Q
    stride = tapers.shape[1] // 2
    half_inner = inner_size // 2
    tm_size = lax.axis_size("tm")
    samples = signal.astype(jnp.float32)
    common = lax.psum(jnp.sum(samples, axis=1), "chan") / (chan_count * lax.axis_size("chan"))
    referenced = (samples - common[:, None]).astype(jnp.bfloat16)
    all_rows = row_count * tm_size
    segments = all_rows // stride - 1
    tables = dft_tables(outer_size, inner_size)
    weights = eigenvalues / jnp.sum(eigenvalues)
    taper_grid = tapers.reshape(tapers.shape[0], inner_size, outer_size, 1, 1)
    columns = lax.all_to_all(referenced, "tm", split_axis=1, concat_axis=0, tiled=True)
    narrow = columns.shape[1]
    widened = columns.astype(jnp.float32)
    centre = jnp.sum(widened, axis=0) / all_rows
    variance = jnp.sum((widened - centre) ** 2, axis=0) / all_rows
    halves = columns.reshape(all_rows // stride, half_inner, outer_size, narrow)
    halves = jnp.transpose(halves, (1, 2, 0, 3))
    windows = jnp.concatenate([halves[:, :, :-1], halves[:, :, 1:]], axis=0)

    def add_column_taper(taper, accumulated):
        taper_row = lax.dynamic_index_in_dim(taper_grid, taper, 0, keepdims=False).astype(
            jnp.float32
        )
        tapered = ((windows.astype(jnp.float32) - centre) * taper_row).astype(jnp.bfloat16)
        power = taper_power(tapered, tables)
        return accumulated + weights[taper] * jnp.sum(power, axis=2).reshape(stride, narrow)

    total = lax.fori_loop(
        0, tapers.shape[0], add_column_taper, jnp.zeros((stride, narrow), jnp.float32)
    )
    density = total / segments / (variance + EPSILON)
    return lax.all_to_all(density, "tm", split_axis=0, concat_axis=1, tiled=True)


def solution(mesh):
    return jax.shard_map(
        local,
        mesh=mesh,
        in_specs=(P("tm", "chan"), P(), P()),
        out_specs=P("tm", "chan"),
        check_vma=False,
    )
```

profile of v0, /device:TPU:0, one launch (start us, length us, event | category | flops | bytes accessed | tf_op | source)
XLA Modules:
  0.0 131.2 jit_solution(6070422819959520975)
XLA Ops:
  0.0 1.5 %copy.30 = bf16[2048,256]{0,1:T(8,128)(2,1)S(1)} copy(bf16[2048,256]{1,0:T(8,128)(2,1)} %param.5) | data formatting | bytes 2097152 | tf_op args[0]
  1.7 5.9 %psum.7 = f32[2048]{0:T(1024)S(1)} all-reduce(f32[2048]{0:T(1024)S(1)} %convert_reduce_fusion.1), channel_id=1, replica_groups=mesh['tm'=16,'chan'=2] {'chan'}, use_global_device_ids=true, to_apply=%region_1.0 | all-reduce | flops 2048 | bytes 16384 | tf_op jit(solution)/shard_map/psum | solution.py:63
  7.6 1.2 fusion.55
  8.8 6.5 %all-to-all-start = ((bf16[2048,16,16]{0,2,1:T(8,128)(2,1)}), bf16[2048,16,16]{0,2,1:T(8,128)(2,1)S(1)}, u32[]{:S(2)}, u32[]{:S(2)}) async-start(bf16[2048,16,16]{0,2,1:T(8,128)(2,1)} %bitcast), calls=%async_computation | async-start | bytes 2097152 | tf_op jit(solution)/shard_map/all_to_all | solution.py:70
  17.4 20.9 %all-to-all-done = bf16[2048,16,16]{0,2,1:T(8,128)(2,1)S(1)} async-done(((bf16[2048,16,16]{0,2,1:T(8,128)(2,1)}), bf16[2048,16,16]{0,2,1:T(8,128)(2,1)S(1)}, u32[]{:S(2)}, u32[]{:S(2)}) %all-to-all-start) | async-done | bytes 1048608 | tf_op jit(solution)/shard_map/all_to_all | solution.py:70
  39.2 4.4 %reshape.113 = bf16[16,64,32,16]{2,1,3,0:T(8,128)(2,1)} reshape(bf16[16,2048,16]{1,2,0:T(8,128)(2,1)S(1)} %bitcast.71) | data formatting | bytes 2097152 | tf_op jit(solution)/shard_map/reshape | solution.py:75
  43.6 7.0 %fusion.64 = (bf16[64,32,15,16]{1,0,3,2:T(8,128)(2,1)}, bf16[64,32,15,16]{1,0,3,2:T(8,128)(2,1)}) fusion(bf16[64,32,16,16]{1,0,3,2:T(8,128)(2,1)} %bitcast.70), kind=kLoop, calls=%fused_computation.89 | loop fusion | bytes 3932160 | tf_op jit(solution)/shard_map/slice | solution.py:77
  50.6 5.8 %copy.31 = bf16[64,32,15,16]{0,3,2,1:T(8,128)(2,1)} copy(bf16[64,32,15,16]{1,0,3,2:T(8,128)(2,1)} %get-tuple-element.308) | data formatting | bytes 1966080 | tf_op jit(solution)/shard_map/slice | solution.py:77
  56.5 5.8 %copy.32 = bf16[64,32,15,16]{0,3,2,1:T(8,128)(2,1)} copy(bf16[64,32,15,16]{1,0,3,2:T(8,128)(2,1)} %get-tuple-element.309) | data formatting | bytes 1966080 | tf_op jit(solution)/shard_map/slice | solution.py:77
  62.2 3.2 %pad_maximum_fusion = bf16[128,32,15,16]{0,3,2,1:T(8,128)(2,1)S(1)} fusion(bf16[64,32,15,16]{0,3,2,1:T(8,128)(2,1)} %copy.32, bf16[64,32,15,16]{0,3,2,1:T(8,128)(2,1)} %copy.31), kind=kLoop, calls=%fused_computation.70 | loop fusion | flops 3932160 | bytes 3932160 | tf_op jit(solution)/shard_map/concatenate | solution.py:77
  65.4 50.4 %while.15 = (s32[]{:T(128)}, f32[2048,16]{0,1:T(8,128)S(1)}, f32[8]{0:T(128)S(1)}, bf16[128,32,15,16]{0,3,2,1:T(8,128)(2,1)S(1)}, f32[16]{0:T(128)S(1)}, /*index...) while((s32[]{:T(128)}, f32[2048,16]{0,1:T(8,128)S(1)}, ...), condition=%wide.region_6.7_spmd.clone.clone, body=%wide.region_4.6_spmd.clone.clone.sunk | while | flops 644048896 | bytes 42246336 | solution.py:87
  66.2 1.2 convolution_bitcast_fusion.2
  67.4 1.1 add_convert_fusion.2
  70.0 0.9 add_reduce_fusion.2
  72.5 1.2 convolution_bitcast_fusion.2
  73.7 1.1 add_convert_fusion.2
  78.8 1.2 convolution_bitcast_fusion.2
  80.0 1.1 add_convert_fusion.2
  82.6 0.9 add_reduce_fusion.2
  85.1 1.2 convolution_bitcast_fusion.2
  86.3 1.1 add_convert_fusion.2
  91.4 1.2 convolution_bitcast_fusion.2
  92.6 1.1 add_convert_fusion.2
  95.2 0.9 add_reduce_fusion.2
  97.7 1.2 convolution_bitcast_fusion.2
  98.9 1.1 add_convert_fusion.2
  104.0 1.2 convolution_bitcast_fusion.2
  105.2 1.1 add_convert_fusion.2
  107.8 0.9 add_reduce_fusion.2
  110.3 1.2 convolution_bitcast_fusion.2
  111.5 1.1 add_convert_fusion.2
  115.9 14.5 %all_to_all.35 = f32[16,128,16]{1,2,0:T(8,128)S(1)} all-to-all(f32[16,128,16]{1,2,0:T(8,128)S(1)} %copy_bitcast_fusion), channel_id=1, replica_groups=mesh['tm'=16,'chan'=2] {'tm'}, dimensions={0} | all-to-all | bytes 262144 | tf_op jit(solution)/shard_map/all_to_all | solution.py:91
  (87 shorter events, 31.6 us)
Async XLA Ops:
  7.6 7.7 %copy-start = (bf16[8,4096]{1,0:T(8,128)(2,1)S(1)}, bf16[8,4096]{1,0:T(8,128)(2,1)}, u32[]{:S(2)}) copy-start(bf16[8,4096]{1,0:T(8,128)(2,1)} %param.6) | copy-start | bytes 196612
  7.6 8.1 %copy-start.1 = (f32[8]{0:T(128)S(1)}, f32[8]{0:T(128)}, u32[]{:S(2)}) copy-start(f32[8]{0:T(128)} %param.7) | copy-start | bytes 100
  8.8 29.4 %all-to-all-start = ((bf16[2048,16,16]{0,2,1:T(8,128)(2,1)}), bf16[2048,16,16]{0,2,1:T(8,128)(2,1)S(1)}, u32[]{:S(2)}, u32[]{:S(2)}) async-start(bf16[2048,16,16]{0,2,1:T(8,128)(2,1)} %bitcast), calls=%async_computation | async-start | bytes 2097152 | tf_op jit(solution)/shard_map/all_to_all | solution.py:70
where the time goes:
time: 132 us; the launch traced here: 131 us
  local copies, waits for them, and re-layouts  30.9 us (23%)
  matrix products  28.8 us (22%)
  other arithmetic  23.2 us (18%)
  waiting for transfers between devices  20.9 us (16%)
  blocking collectives  20.4 us (15%)
  starting transfers between devices  6.47 us (5%)
    all_to_all x1, waiting for transfers between devices, local(): lax.all_to_all(referenced, 'tm', split_axis=1, concat_axis=0, tiled=True)  20.9 us
    slice x3, local copies, waits for them, and re-layouts, local(): windows = jnp.concatenate([halves[:, :, :-1], halves[:, :, 1:]], axis=0)  18.6 us
    all_to_all x1, blocking collectives, local(): lax.all_to_all(density, 'tm', split_axis=0, concat_axis=1, tiled=True)  14.5 us
    dot_general x8, matrix products, taper_power(): jnp.einsum('jn,npsc->jpsc', first_table, tapered, preferred_element_type=...  9.85 us
    convert_element_type x8, other arithmetic, taper_power(): (first_real * twist_cos + first_imaginary * twist_sin).astype(jnp.bfloat16)  8.88 us
    dot_general x8, matrix products, taper_power(): jnp.einsum('pa,kpsc->aksc', last_sin, twist_real, preferred_element_type=...  7.2 us
    all_to_all x1, starting transfers between devices, local(): lax.all_to_all(referenced, 'tm', split_axis=1, concat_axis=0, tiled=True)  6.47 us
    psum x1, blocking collectives, local(): lax.psum(jnp.sum(samples, axis=1), 'chan')  5.94 us
  transfers between devices with their start and end apart: 1, of which 1 were waited for; matrix products, arithmetic and copies ran while one was open for 2% of the time, Pallas kernels for 0%

commit v1 on v0

v1 whole, which is shorter than its diff:
```python
import math

import jax
import jax.numpy as jnp
import numpy as np
from jax import lax
from jax.experimental import pallas as pl
from jax.experimental.pallas import tpu as pltpu
from jax.sharding import PartitionSpec as P

EPSILON = 1e-06
LANES = 128
R = 32
UNITS = R // 2
f32 = jnp.float32
bf16 = jnp.bfloat16

CONJ = {3: 29, 7: 25, 11: 21, 15: 17, 6: 26, 14: 18}


def unit_tables(seg, groups):
    half_m = seg // 2 // R
    per = half_m // groups
    n1 = np.arange(LANES)[:, None]
    col = np.arange(LANES)
    d = col // (2 * per)
    s = (col // per) % 2
    q = col % per
    m = d * per + q
    out = np.zeros((UNITS, 2 * LANES, 2 * LANES), np.float64)
    for u in range(UNITS):
        if u == 0:
            k = R * m + s * (R // 2)
            ang = 2 * np.pi * ((n1 * k) % seg) / seg
            for part in range(2):
                pick = (s == part)[None, :]
                rows = slice(part * LANES, (part + 1) * LANES)
                out[u, rows, :LANES] = np.cos(ang) * pick
                out[u, rows, LANES:] = -np.sin(ang) * pick
        else:
            k = np.where(s == 0, R * m + u, seg - (R * m + R - u))
            ang = 2 * np.pi * ((n1 * k) % seg) / seg
            sign = -1.0 if u in CONJ else 1.0
            out[u, :LANES, :LANES] = np.cos(ang)
            out[u, :LANES, LANES:] = -np.sin(ang)
            out[u, LANES:, :LANES] = sign * np.sin(ang)
            out[u, LANES:, LANES:] = sign * np.cos(ang)
    return out.astype(np.float32).astype(jnp.bfloat16)


def bin_rows(groups, seg):
    per = seg // 2 // R // groups
    rows = []
    for q in range(per):
        for b in range(R):
            if b < UNITS:
                u, s = b, 0
            elif b == UNITS:
                u, s = 0, 1
            else:
                u, s = R - b, 1
            rows.append(u * 2 * per + s * per + q)
    return rows


def cmul(a, angle):
    re, im = a
    c, s = math.cos(angle), math.sin(angle)
    return (re * c + im * s, im * c - re * s)


def rot45(a):
    h = math.sqrt(0.5)
    re, im = a
    return ((re + im) * h, (im - re) * h)


def rot135(a):
    h = math.sqrt(0.5)
    re, im = a
    return ((im - re) * h, (re + im) * -h)


def cadd(a, b):
    return (a[0] + b[0], a[1] + b[1])


def csub(a, b):
    return (a[0] - b[0], a[1] - b[1])


def fft4(c):
    e0, e1 = cadd(c[0], c[2]), csub(c[0], c[2])
    o0, o1 = cadd(c[1], c[3]), csub(c[1], c[3])
    return [
        cadd(e0, o0),
        (e1[0] + o1[1], e1[1] - o1[0]),
        csub(e0, o0),
        (e1[0] - o1[1], e1[1] + o1[0]),
    ]


def real_fft32(x, put):
    s0, s1, s2 = [], [], []
    for a in range(8):
        p, m = x[a] + x[a + 16], x[a] - x[a + 16]
        pb, mb = x[a + 8] + x[a + 24], x[a + 8] - x[a + 24]
        s0.append(p + pb)
        s2.append(p - pb)
        s1.append((m, mb))
    h = math.sqrt(0.5)
    t = [s0[n] + s0[n + 4] for n in range(4)]
    v = [s0[n] - s0[n + 4] for n in range(4)]
    e, o = t[0] + t[2], t[1] + t[3]
    put(0, e + o, e - o)
    put(8, t[0] - t[2], t[3] - t[1])
    a1, a3 = (v[1] - v[3]) * h, (v[1] + v[3]) * h
    put(4, v[0] + a1, -v[2] - a3)
    put(12, v[0] - a1, v[2] - a3)
    w = -2 * math.pi / 16
    c = [(s2[0], -s2[4])]
    for n in range(1, 4):
        c.append((s2[n], s2[n + 4]))

    def rotated(n):
        a, b = c[n]
        cs, sn = math.cos(2 * math.pi * n / 16), math.sin(2 * math.pi * n / 16)
        if n == 2:
            return ((a - b) * h, (a + b) * -h)
        return (a * cs - b * sn, a * -sn - b * cs)

    f = fft4([c[0], rotated(1), rotated(2), rotated(3)])
    put(2, *f[0])
    put(10, *f[1])
    put(14, *f[2])
    put(6, *f[3])
    g = [(s1[0][0], -s1[0][1])]
    for n in range(1, 8):
        a, b = s1[n]
        if n == 4:
            g.append(((a - b) * h, (a + b) * -h))
        else:
            cs, sn = math.cos(2 * math.pi * n / 32), math.sin(2 * math.pi * n / 32)
            g.append((a * cs - b * sn, a * -sn - b * cs))
    even = fft4([g[0], g[2], g[4], g[6]])
    odd = fft4([g[1], g[3], g[5], g[7]])
    o0 = odd[0]
    o1 = rot45(odd[1])
    o3 = rot135(odd[3])
    o2 = odd[2]
    put(1, *cadd(even[0], o0))
    put(15, *csub(even[0], o0))
    put(5, *cadd(even[1], o1))
    put(11, *csub(even[1], o1))
    put(9, even[2][0] + o2[1], even[2][1] - o2[0])
    put(7, even[2][0] - o2[1], even[2][1] + o2[0])
    put(13, *cadd(even[3], o3))
    put(3, *csub(even[3], o3))


def prep_kernel(own_ref, near_ref, common_ref, ref_ref, stats_ref):
    blocks = own_ref.shape[0] // LANES
    count = 2 * blocks * LANES

    def block(b, total):
        for h, src in enumerate((own_ref, near_ref)):
            x = src[pl.ds(pl.multiple_of(b * LANES, LANES), LANES), :].astype(f32).T
            x = (x - common_ref[h, pl.ds(b, 1), :]).astype(bf16)
            ref_ref[h, b] = x
            total = total + x.astype(f32)
        return total

    total = lax.fori_loop(0, blocks, block, jnp.zeros((LANES, LANES), f32))
    mean = jnp.sum(total, axis=1, keepdims=True) / count
    mean_wide = jnp.broadcast_to(mean, (LANES, LANES))

    def spread(b, acc):
        for h in range(2):
            d = ref_ref[h, b].astype(f32) - mean_wide
            acc = acc + d * d
        return acc

    acc = lax.fori_loop(0, blocks, spread, jnp.zeros((LANES, LANES), f32))
    stats_ref[0:1, :] = mean_wide.T[0:1, :]
    stats_ref[1:2, :] = jnp.sum(acc.T, axis=0, keepdims=True)


def main_kernel(order_ref, ref_ref, far_ref, far_common_ref, centre_ref, scale_ref, taps_ref,
                w_ref, out_ref, y_ref, ga_ref, gb_ref, acc_ref):
    blocks = ref_ref.shape[1]
    tapers = taps_ref.shape[1]
    groups = out_ref.shape[0]
    rows_per = LANES // groups
    chunks = 2 * LANES // 16
    centre = jnp.broadcast_to(centre_ref[...], (LANES, LANES)).T

    own_at = blocks
    near_at = order_ref[0] * blocks
    far_at = order_ref[1] * blocks

    def prepare(b, _):
        y_ref[own_at + b] = ref_ref[0, b].astype(f32) - centre
        y_ref[near_at + b] = ref_ref[1, b].astype(f32) - centre
        x = far_ref[pl.ds(pl.multiple_of(b * LANES, LANES), LANES), :].astype(f32).T
        x = (x - far_common_ref[pl.ds(b, 1), :]).astype(bf16).astype(f32)
        y_ref[far_at + b] = x - centre
        return 0

    lax.fori_loop(0, blocks, prepare, 0)
    acc_ref[...] = jnp.zeros(acc_ref.shape, f32)

    def first(r, taper, dst):
        seg = r // (chunks // 2)
        at = pl.multiple_of((r % (chunks // 2)) * 16, 16)
        row = pl.multiple_of(r * 16, 16)
        x = [
            y_ref[blocks * seg + n, pl.ds(at, 16), :] * taps_ref[seg, taper, n : n + 1, :]
            for n in range(R)
        ]

        def put(u, re, im):
            dst[u, pl.ds(row, 16), :LANES] = re.astype(bf16)
            dst[u, pl.ds(row, 16), LANES:] = im.astype(bf16)

        real_fft32(x, put)

    def second(u, src):
        z = jnp.dot(src[u], w_ref[u], preferred_element_type=f32)
        p = z * z
        p = p[:, :LANES] + p[:, LANES:]
        acc_ref[u] += p[:LANES] + p[LANES:]

    def both(taper, src, dst):
        def body(i, _):
            second(i, src)
            first(i, taper + 1, dst)
            return 0

        lax.fori_loop(0, UNITS, body, 0)

    def start(i, _):
        first(i, 0, ga_ref)
        return 0

    lax.fori_loop(0, chunks, start, 0)

    def pair(i, _):
        both(2 * i, ga_ref, gb_ref)
        both(2 * i + 1, gb_ref, ga_ref)
        return 0

    lax.fori_loop(0, tapers // 2 - 1, pair, 0)
    both(tapers - 2, ga_ref, gb_ref)

    def last(u, _):
        second(u, gb_ref)
        return 0

    lax.fori_loop(0, UNITS, last, 0)

    for u in range(UNITS):
        t = (acc_ref[u].T * scale_ref[...]).astype(bf16)
        for d in range(groups):
            out_ref[d, u * rows_per : (u + 1) * rows_per, :] = t[d * rows_per : (d + 1) * rows_per]


def merge_kernel(rows, parts_ref, out_ref, sum_ref):
    groups = parts_ref.shape[0]
    for parity in range(2):
        total = parts_ref[parity].astype(f32)
        for g in range(parity + 2, groups, 2):
            total = total + parts_ref[g].astype(f32)
        sum_ref[:, parity * LANES : (parity + 1) * LANES] = total
    for i, r in enumerate(rows):
        out_ref[i : i + 1, :] = sum_ref[r : r + 1, :]


def local(signal, tapers, eigenvalues):
    row_count, chan_count = signal.shape
    taper_count, seg = tapers.shape
    stride = seg // 2
    tm = lax.axis_size("tm")
    chans = lax.axis_size("chan")
    blocks = row_count // LANES
    all_rows = row_count * tm
    segments = all_rows // stride - 1
    half = chan_count // 2
    assert row_count == stride and half == LANES and seg == R * LANES
    index = lax.axis_index("tm")
    parity = index % 2

    near = [(i, i ^ 1) for i in range(tm)]
    far = [(i, i + 1 if i % 2 else i - 1) for i in range(1, tm - 1)]

    keep = lax.dynamic_slice_in_dim(signal, parity * half, half, 1)
    send = lax.dynamic_slice_in_dim(signal, (1 - parity) * half, half, 1)
    near_raw = lax.ppermute(send, "tm", near)
    far_raw = lax.ppermute(send, "tm", far)

    sums = jnp.sum(signal.astype(f32), axis=1).reshape(blocks, LANES)
    if chans == 2:
        total = sums + lax.ppermute(sums, "chan", [(0, 1), (1, 0)])
    else:
        total = lax.psum(sums, "chan")
    common = total / (chan_count * chans)
    common_near = lax.ppermute(common, "tm", near)
    common_far = lax.ppermute(common, "tm", far)

    referenced, stats = pl.pallas_call(
        prep_kernel,
        out_shape=(
            jax.ShapeDtypeStruct((2, blocks, LANES, LANES), bf16),
            jax.ShapeDtypeStruct((2, LANES), f32),
        ),
        name="prep",
    )(keep, near_raw, jnp.stack([common, common_near]))

    mean, spread = stats[0], stats[1]
    count = 2 * row_count
    step = 2
    while step < tm:
        other = lax.ppermute(jnp.stack([mean, spread]), "tm", [(i, i ^ step) for i in range(tm)])
        gap = other[0] - mean
        mean = (mean + other[0]) * 0.5
        spread = spread + other[1] + gap * gap * (count * 0.5)
        count *= 2
        step *= 2
    variance = spread / all_rows
    scale = 1.0 / (segments * (variance + EPSILON))

    weights = eigenvalues / jnp.sum(eigenvalues)
    valid = jnp.stack([index > 0, index < tm - 1]).astype(f32)
    taps = tapers.astype(f32) * jnp.sqrt(weights)[:, None]
    taps = (valid[:, None, None] * taps[None]).reshape(2, taper_count, R, LANES)
    order = jnp.stack([2 * (1 - parity), 2 * parity]).astype(jnp.int32)
    table = jnp.asarray(unit_tables(seg, tm))

    vmem = pl.BlockSpec(memory_space=pltpu.VMEM)
    parts = pl.pallas_call(
        main_kernel,
        out_shape=jax.ShapeDtypeStruct((tm, stride // tm, LANES), bf16),
        in_specs=[pl.BlockSpec(memory_space=pltpu.SMEM)] + [vmem] * 7,
        out_specs=vmem,
        scratch_shapes=[
            pltpu.VMEM((3 * blocks, LANES, LANES), f32),
            pltpu.VMEM((UNITS, 2 * LANES, 2 * LANES), bf16),
            pltpu.VMEM((UNITS, 2 * LANES, 2 * LANES), bf16),
            pltpu.VMEM((UNITS, LANES, LANES), f32),
        ],
        name="spectra",
    )(order, referenced, far_raw, common_far, mean[None], scale[None], taps, table)

    got = lax.all_to_all(parts, "tm", 0, 0, tiled=True)
    rows = bin_rows(tm, seg)
    return pl.pallas_call(
        lambda *refs: merge_kernel(rows, *refs),
        out_shape=jax.ShapeDtypeStruct((stride // tm, chan_count), f32),
        scratch_shapes=[pltpu.VMEM((stride // tm, chan_count), f32)],
        name="merge",
    )(got)


def solution(mesh):
    return jax.shard_map(
        local,
        mesh=mesh,
        in_specs=(P("tm", "chan"), P(), P()),
        out_specs=P("tm", "chan"),
        check_vma=False,
    )
```

time: 132 us -> 89 us (0.67)
  Pallas kernels: 0 us -> 39.5 us
  matrix products: 28.8 us -> 0 us
  local copies, waits for them, and re-layouts: 30.9 us -> 3.83 us
  other arithmetic: 23.2 us -> 5.07 us
  waiting for transfers between devices: 20.9 us -> 4.21 us
  starting transfers between devices: 6.47 us -> 14.4 us
    pallas_call x0 -> x3, Pallas kernels: none -> 39.5 us  [the longest x1 33.3 us: local(): pl.pallas_call(main_kernel, out_shape=jax.ShapeDtypeStruct((tm, stride //...]
    dot_general x40 -> x0, matrix products: 28.8 us -> none  [the longest x8 9.85 us: taper_power(): jnp.einsum('jn,npsc->jpsc', first_table, tapered, preferred_element_type=...]
    all_to_all x1 -> x0, waiting for transfers between devices: 20.9 us -> none  [local(): lax.all_to_all(referenced, 'tm', split_axis=1, concat_axis=0, tiled=True)]
    slice x3 -> x0, local copies, waits for them, and re-layouts: 18.6 us -> none  [local(): windows = jnp.concatenate([halves[:, :, :-1], halves[:, :, 1:]], axis=0)]
    ppermute x0 -> x8, starting transfers between devices: none -> 14.4 us  [the longest x3 7.61 us: local(): lax.ppermute(jnp.stack([mean, spread]), 'tm', [(i, i ^ step) for i in ran...]
    convert_element_type x17 -> x1, other arithmetic: 10.1 us -> 0.08 us  [local(): valid = jnp.stack([index > 0, index < tm - 1]).astype(f32)]
    all_to_all x1, blocking collectives: 14.5 us -> 21.6 us  [local(): got = lax.all_to_all(parts, 'tm', 0, 0, tiled=True)]
    all_to_all x1 -> x0, starting transfers between devices: 6.47 us -> none  [local(): lax.all_to_all(referenced, 'tm', split_axis=1, concat_axis=0, tiled=True)]
  transfers between devices with their start and end apart: 1 -> 8, of which waited for: 1 -> 5; matrix products, arithmetic and copies ran while one was open for 2% -> 6% of each run, Pallas kernels for 0% -> 5%
where the time goes in v1:
time: 89 us; the launch traced here: 88.6 us
  Pallas kernels  39.5 us (44%)
  blocking collectives  21.6 us (24%)
  starting transfers between devices  14.4 us (16%)
  other arithmetic  5.07 us (6%)
  waiting for transfers between devices  4.21 us (5%)
  local copies, waits for them, and re-layouts  3.83 us (4%)
    pallas_call x1, Pallas kernels, local(): pl.pallas_call(main_kernel, out_shape=jax.ShapeDtypeStruct((tm, stride //...  33.3 us
    all_to_all x1, blocking collectives, local(): got = lax.all_to_all(parts, 'tm', 0, 0, tiled=True)  21.6 us
    ppermute x3, starting transfers between devices, local(): lax.ppermute(jnp.stack([mean, spread]), 'tm', [(i, i ^ step) for i in ran...  7.61 us
    pallas_call x1, Pallas kernels, local(): pl.pallas_call(prep_kernel, out_shape=(jax.ShapeDtypeStruct((2, blocks, L...  4.37 us
    ppermute x3, waiting for transfers between devices, local(): lax.ppermute(jnp.stack([mean, spread]), 'tm', [(i, i ^ step) for i in ran...  3.11 us
    ppermute x1, starting transfers between devices, local(): total = sums + lax.ppermute(sums, 'chan', [(0, 1), (1, 0)])  2.54 us
    ppermute x1, starting transfers between devices, local(): common_near = lax.ppermute(common, 'tm', near)  2.38 us
    dynamic_slice x1, local copies, waits for them, and re-layouts, local(): send = lax.dynamic_slice_in_dim(signal, (1 - parity) * half, half, 1)  2.19 us
  transfers between devices with their start and end apart: 8, of which 5 were waited for; matrix products, arithmetic and copies ran while one was open for 6% of the time, Pallas kernels for 5%

profile of v1, /device:TPU:0, one launch (start us, length us, event | category | flops | bytes accessed | tf_op | source)
XLA Modules:
  0.0 88.6 jit_solution(6087227120868624875)
XLA Ops:
  0.0 2.2 %constant_dynamic-slice_fusion = (bf16[2048,128]{1,0:T(8,128)(2,1)S(1)}, bf16[2048,128]{1,0:T(8,128)(2,1)}) fusion(bf16[2048,256]{1,0:T(8,128)(2,1)} %param.4, s32[]{:T(128)S(6)} %select_n.15, s32[]{:T(128)S(6)} %select_n.14), kind=kLoop, calls=%fused_computation.16 | loop fusion | bytes 2097160 | tf_op jit(solution)/shard_map/dynamic_slice | solution.py:296
  2.2 0.5 collective-permute-start
  2.7 0.7 collective-permute-start.3
  3.4 0.3 convert_reduce_fusion
  3.8 2.5 %collective-permute-start.1 = (f32[16,128]{1,0:T(8,128)S(1)}, f32[16,128]{1,0:T(8,128)S(1)}, u32[]{:S(2)}, u32[]{:S(2)}) collective-permute-start(f32[16,128]{1,0:T(8,128)S(1)} %bitcast.13), channel_id=1, source_target_pairs={{0,1},{1,0},{2,3},{3,2},{4,5},{5,4},{6,7},{7,6},{8,9},{9,8},{10,11... | collective-permute-start | bytes 24584 | tf_op jit(solution)/shard_map/ppermute | solution.py:302
  6.3 0.6 reduce_sum.19
  6.9 0.7 divide_sqrt_fusion
  7.6 0.1 multiply_bitcast_fusion
  7.7 0.3 collective-permute-done.1
  7.9 2.4 %collective-permute-start.2 = (f32[16,128]{1,0:T(8,128)S(1)}, f32[16,128]{1,0:T(8,128)S(1)}, u32[]{:S(2)}, u32[]{:S(2)}) collective-permute-start(f32[16,128]{1,0:T(8,128)S(1)} %add_multiply_fusion), channel_id=1, source_target_pairs={{0,2},{2,0},{4,6},{6,4},{8,10},{10,8},{12,14},{14,12},{16,18},{18,... | collective-permute-start | bytes 24584 | tf_op jit(solution)/shard_map/ppermute | solution.py:306
  10.3 0.8 collective-permute-done.2
  11.2 0.6 pad_maximum_fusion.common_ref
  11.8 0.0 collective-permute-done.near_ref
  11.8 0.8 copy-done.1
  12.6 4.4 %prep.1 = (bf16[2,16,128,128]{3,2,1,0:T(8,128)(2,1)}, f32[2,128]{1,0:T(2,128)}) custom-call(bf16[2048,128]{1,0:T(8,128)(2,1)} %get-tuple-element.10.own_ref, bf16[2048,128]{1,0:T(8,128)(2,1)} %copy-done.1, f32[2,16,128]{2,1,0:T(8,128)} %pad_maximum_fusion.common_ref), custom_call_target="tpu_custom_call" | custom-call | tf_op jit(solution)/shard_map/prep/pallas_call | solution.py:309
  16.9 1.7 %collective-permute-start.5 = (f32[2,128]{1,0:T(2,128)}, f32[2,128]{1,0:T(2,128)S(1)}, u32[]{:S(2)}, u32[]{:S(2)}) collective-permute-start(f32[2,128]{1,0:T(2,128)} %get-tuple-element.8), channel_id=1, source_target_pairs={{0,4},{2,6},{4,0},{6,2},{8,12},{10,14},{12,8},{14,10},{16,20},{18,... | collective-permute-start | bytes 3080 | tf_op jit(solution)/shard_map/ppermute | solution.py:322
  18.6 0.1 add_convert_fusion
  18.7 2.0 %collective-permute-done.5 = f32[2,128]{1,0:T(2,128)S(1)} collective-permute-done((f32[2,128]{1,0:T(2,128)}, f32[2,128]{1,0:T(2,128)S(1)}, u32[]{:S(2)}, u32[]{:S(2)}) %collective-permute-start.5) | collective-permute-done | bytes 1056 | tf_op jit(solution)/shard_map/ppermute | solution.py:322
  20.7 0.7 multiply_add_fusion.1
  21.5 2.9 %collective-permute-start.6 = (f32[2,128]{1,0:T(2,128)S(1)}, f32[2,128]{1,0:T(2,128)S(1)}, u32[]{:S(2)}, u32[]{:S(2)}) collective-permute-start(f32[2,128]{1,0:T(2,128)S(1)} %pad_maximum_fusion.1), channel_id=1, source_target_pairs={{0,8},{2,10},{4,12},{6,14},{8,0},{10,2},{12,4},{14,6},{16,24},{18,... | collective-permute-start | bytes 3080 | tf_op jit(solution)/shard_map/ppermute | solution.py:322
  24.3 0.8 broadcast_multiply_fusion.taps_ref
  25.1 0.8 collective-permute-done.6
  25.9 3.1 %collective-permute-start.7 = (f32[2,128]{1,0:T(2,128)S(1)}, f32[2,128]{1,0:T(2,128)S(1)}, u32[]{:S(2)}, u32[]{:S(2)}) collective-permute-start(f32[2,128]{1,0:T(2,128)S(1)} %pad_maximum_fusion.2), channel_id=1, source_target_pairs={{0,16},{2,18},{4,20},{6,22},{8,24},{10,26},{12,28},{14,30},{16,0},... | collective-permute-start | bytes 3080 | tf_op jit(solution)/shard_map/ppermute | solution.py:322
  29.0 0.6 pad_add_fusion.order_ref
  29.6 0.6 collective-permute-start.4
  30.2 0.3 collective-permute-done.7
  30.5 0.6 multiply_divide_fusion
  31.2 0.6 copy-done.4
  31.7 0.2 copy-done.2
  32.0 33.3 %spectra.1 = bf16[16,128,128]{2,1,0:T(8,128)(2,1)} custom-call(s32[2]{0:T(128)} %pad_add_fusion.order_ref, bf16[2,16,128,128]{3,2,1,0:T(8,128)(2,1)} %get-tuple-element.7.ref_ref, bf16[2048,128]{1,0:T(8,128)(2,1)} %copy-done.2, f32[16,128]{1,0:T(8,128)} %copy-done.4, f32[1,128]{1,0:T(1,128)} %get-tuple-element.14.centre_ref, ...), custom_call_target="tpu_custom_call" | custom-call | tf_op jit(solution)/shard_map/spectra/pallas_call | solution.py:339
  65.2 21.6 %all_to_all.5.refs_0_ = bf16[16,128,128]{2,1,0:T(8,128)(2,1)} all-to-all(bf16[16,128,128]{2,1,0:T(8,128)(2,1)} %spectra.1), channel_id=1, replica_groups=mesh['tm'=16,'chan'=2] {'tm'}, dimensions={0} | all-to-all | bytes 1048576 | tf_op jit(solution)/shard_map/all_to_all | solution.py:353
  86.8 1.8 %merge.1 = f32[128,256]{1,0:T(8,128)} custom-call(bf16[16,128,128]{2,1,0:T(8,128)(2,1)} %all_to_all.5.refs_0_), custom_call_target="tpu_custom_call" | custom-call | tf_op jit(solution)/shard_map/merge/pallas_call | solution.py:355
  (17 shorter events, 0.1 us)
Async XLA Ops:
  0.0 3.4 %copy-start = (bf16[2048,256]{1,0:T(8,128)(2,1)S(1)}, bf16[2048,256]{1,0:T(8,128)(2,1)}, u32[]{:S(2)}) copy-start(bf16[2048,256]{1,0:T(8,128)(2,1)} %param.4) | copy-start | bytes 3145732
  0.0 6.3 %copy-start.5 = (f32[8]{0:T(128)S(1)}, f32[8]{0:T(128)}, u32[]{:S(2)}) copy-start(f32[8]{0:T(128)} %param.6) | copy-start | bytes 100
  0.0 7.6 %copy-start.3 = (bf16[8,4096]{1,0:T(8,128)(2,1)S(1)}, bf16[8,4096]{1,0:T(8,128)(2,1)}, u32[]{:S(2)}) copy-start(bf16[8,4096]{1,0:T(8,128)(2,1)} %param.5) | copy-start | bytes 196612
  2.2 9.6 %collective-permute-start = (bf16[2048,128]{1,0:T(8,128)(2,1)S(1)}, bf16[2048,128]{1,0:T(8,128)(2,1)S(1)}, u32[]{:S(2)}, u32[]{:S(2)}) collective-permute-start(bf16[2048,128]{1,0:T(8,128)(2,1)S(1)} %get-tuple-element.9), channel_id=1, source_target_pairs={{0,2},{2,0},{4,6},{6,4},{8,10},{10,8},{12,14},{14,12},{16,18},{18,... | collective-permute-start | bytes 1572872 | tf_op jit(solution)/shard_map/ppermute | solution.py:297
  2.7 28.4 %collective-permute-start.3 = (bf16[2048,128]{1,0:T(8,128)(2,1)S(1)}, bf16[2048,128]{1,0:T(8,128)(2,1)S(1)}, u32[]{:S(2)}, u32[]{:S(2)}) collective-permute-start(bf16[2048,128]{1,0:T(8,128)(2,1)S(1)} %get-tuple-element.9), channel_id=1, source_target_pairs={{2,4},{4,2},{6,8},{8,6},{10,12},{12,10},{14,16},{16,14},{18,20},{2... | collective-permute-start | bytes 1572872 | tf_op jit(solution)/shard_map/ppermute | solution.py:298
  3.8 4.2 %collective-permute-start.1 = (f32[16,128]{1,0:T(8,128)S(1)}, f32[16,128]{1,0:T(8,128)S(1)}, u32[]{:S(2)}, u32[]{:S(2)}) collective-permute-start(f32[16,128]{1,0:T(8,128)S(1)} %bitcast.13), channel_id=1, source_target_pairs={{0,1},{1,0},{2,3},{3,2},{4,5},{5,4},{6,7},{7,6},{8,9},{9,8},{10,11... | collective-permute-start | bytes 24584 | tf_op jit(solution)/shard_map/ppermute | solution.py:302
  7.9 3.2 %collective-permute-start.2 = (f32[16,128]{1,0:T(8,128)S(1)}, f32[16,128]{1,0:T(8,128)S(1)}, u32[]{:S(2)}, u32[]{:S(2)}) collective-permute-start(f32[16,128]{1,0:T(8,128)S(1)} %add_multiply_fusion), channel_id=1, source_target_pairs={{0,2},{2,0},{4,6},{6,4},{8,10},{10,8},{12,14},{14,12},{16,18},{18,... | collective-permute-start | bytes 24584 | tf_op jit(solution)/shard_map/ppermute | solution.py:306
  11.8 0.8 copy-start.1
  16.9 3.8 %collective-permute-start.5 = (f32[2,128]{1,0:T(2,128)}, f32[2,128]{1,0:T(2,128)S(1)}, u32[]{:S(2)}, u32[]{:S(2)}) collective-permute-start(f32[2,128]{1,0:T(2,128)} %get-tuple-element.8), channel_id=1, source_target_pairs={{0,4},{2,6},{4,0},{6,2},{8,12},{10,14},{12,8},{14,10},{16,20},{18,... | collective-permute-start | bytes 3080 | tf_op jit(solution)/shard_map/ppermute | solution.py:322
  21.5 4.4 %collective-permute-start.6 = (f32[2,128]{1,0:T(2,128)S(1)}, f32[2,128]{1,0:T(2,128)S(1)}, u32[]{:S(2)}, u32[]{:S(2)}) collective-permute-start(f32[2,128]{1,0:T(2,128)S(1)} %pad_maximum_fusion.1), channel_id=1, source_target_pairs={{0,8},{2,10},{4,12},{6,14},{8,0},{10,2},{12,4},{14,6},{16,24},{18,... | collective-permute-start | bytes 3080 | tf_op jit(solution)/shard_map/ppermute | solution.py:322
  25.9 4.6 %collective-permute-start.7 = (f32[2,128]{1,0:T(2,128)S(1)}, f32[2,128]{1,0:T(2,128)S(1)}, u32[]{:S(2)}, u32[]{:S(2)}) collective-permute-start(f32[2,128]{1,0:T(2,128)S(1)} %pad_maximum_fusion.2), channel_id=1, source_target_pairs={{0,16},{2,18},{4,20},{6,22},{8,24},{10,26},{12,28},{14,30},{16,0},... | collective-permute-start | bytes 3080 | tf_op jit(solution)/shard_map/ppermute | solution.py:322
  29.6 1.6 %collective-permute-start.4 = (f32[16,128]{1,0:T(8,128)S(1)}, f32[16,128]{1,0:T(8,128)S(1)}, u32[]{:S(2)}, u32[]{:S(2)}) collective-permute-start(f32[16,128]{1,0:T(8,128)S(1)} %add_multiply_fusion), channel_id=1, source_target_pairs={{2,4},{4,2},{6,8},{8,6},{10,12},{12,10},{14,16},{16,14},{18,20},{2... | collective-permute-start | bytes 24584 | tf_op jit(solution)/shard_map/ppermute | solution.py:307
  31.1 0.6 copy-start.4
  31.2 0.8 copy-start.2

commit v2 on v1

--- a/solution.py
+++ b/solution.py
@@ -1,3 +1,4 @@
+import functools
 import math
 
 import jax
@@ -12,6 +13,7 @@
 LANES = 128
 R = 32
 UNITS = R // 2
+UNROLL = 8
 f32 = jnp.float32
 bf16 = jnp.bfloat16
 
@@ -158,55 +160,70 @@
     put(3, *csub(even[3], o3))
 
 
-def prep_kernel(own_ref, near_ref, common_ref, ref_ref, stats_ref):
-    blocks = own_ref.shape[0] // LANES
-    count = 2 * blocks * LANES
-
-    def block(b, total):
-        for h, src in enumerate((own_ref, near_ref)):
-            x = src[pl.ds(pl.multiple_of(b * LANES, LANES), LANES), :].astype(f32).T
-            x = (x - common_ref[h, pl.ds(b, 1), :]).astype(bf16)
-            ref_ref[h, b] = x
+def prep_kernel(signal_ref, common_ref, keep_ref, send_ref, keep_stats_ref, send_stats_ref):
+    parity = lax.axis_index("tm") % 2
+    blocks = keep_ref.shape[0]
+    count = blocks * LANES
+    sides = ((parity, keep_ref, keep_stats_ref), (1 - parity, send_ref, send_stats_ref))
+    for side, dst, stats in sides:
+        lanes = pl.ds(pl.multiple_of(side * LANES, LANES), LANES)
+        total = jnp.zeros((LANES, LANES), f32)
+        for b in range(blocks):
+            x = signal_ref[b * LANES : (b + 1) * LANES, lanes].astype(f32).T
+            x = (x - common_ref[b : b + 1, :]).astype(bf16)
+            dst[b] = x
             total = total + x.astype(f32)
-        return total
-
-    total = lax.fori_loop(0, blocks, block, jnp.zeros((LANES, LANES), f32))
-    mean = jnp.sum(total, axis=1, keepdims=True) / count
-    mean_wide = jnp.broadcast_to(mean, (LANES, LANES))
-
-    def spread(b, acc):
-        for h in range(2):
-            d = ref_ref[h, b].astype(f32) - mean_wide
-            acc = acc + d * d
-        return acc
-
-    acc = lax.fori_loop(0, blocks, spread, jnp.zeros((LANES, LANES), f32))
-    stats_ref[0:1, :] = mean_wide.T[0:1, :]
-    stats_ref[1:2, :] = jnp.sum(acc.T, axis=0, keepdims=True)
-
-
-def main_kernel(order_ref, ref_ref, far_ref, far_common_ref, centre_ref, scale_ref, taps_ref,
-                w_ref, out_ref, y_ref, ga_ref, gb_ref, acc_ref):
-    blocks = ref_ref.shape[1]
+        mean = jnp.sum(total, axis=1, keepdims=True) / count
+        mean_wide = jnp.broadcast_to(mean, (LANES, LANES))
+
+        def spread(b, acc):
+            d = dst[b].astype(f32) - mean_wide
+            return acc + d * d
+
+        acc = lax.fori_loop(0, blocks, spread, jnp.zeros((LANES, LANES), f32))
+        stats[0:1, :] = mean_wide.T[0:1, :]
+        stats[1:2, :] = jnp.sum(acc.T, axis=0, keepdims=True)
+
+
+def main_kernel(segments, count, keep_ref, near_ref, far_ref, *refs):
+    stats_refs = refs[:-8]
+    taps_in_ref, w_ref, out_ref, taps_ref, y_ref, ga_ref, gb_ref, acc_ref = refs[-8:]
+    index = lax.axis_index("tm")
+    parity = index % 2
+    blocks = keep_ref.shape[0]
     tapers = taps_ref.shape[1]
     groups = out_ref.shape[0]
     rows_per = LANES // groups
     chunks = 2 * LANES // 16
-    centre = jnp.broadcast_to(centre_ref[...], (LANES, LANES)).T
-
-    own_at = blocks
-    near_at = order_ref[0] * blocks
-    far_at = order_ref[1] * blocks
-
-    def prepare(b, _):
-        y_ref[own_at + b] = ref_ref[0, b].astype(f32) - centre
-        y_ref[near_at + b] = ref_ref[1, b].astype(f32) - centre
-        x = far_ref[pl.ds(pl.multiple_of(b * LANES, LANES), LANES), :].astype(f32).T
-        x = (x - far_common_ref[pl.ds(b, 1), :]).astype(bf16).astype(f32)
-        y_ref[far_at + b] = x - centre
+
+    parts = len(stats_refs)
+    mean = stats_refs[0][0:1, :]
+    for ref in stats_refs[1:]:
+        mean = mean + ref[0:1, :]
+    mean = mean / parts
+    spread = jnp.zeros((1, LANES), f32)
+    for ref in stats_refs:
+        gap = ref[0:1, :] - mean
+        spread = spread + ref[1:2, :] + gap * gap * count
+    scale = 1.0 / (segments * (spread / (count * parts) + EPSILON))
+    centre = jnp.broadcast_to(mean, (LANES, LANES)).T
+
+    near_at = 2 * (1 - parity) * blocks
+    far_at = 2 * parity * blocks
+
+    def prepare(i, _):
+        for j in range(4):
+            b = 4 * i + j
+            y_ref[blocks + b] = keep_ref[b].astype(f32) - centre
+            y_ref[near_at + b] = near_ref[b].astype(f32) - centre
+            y_ref[far_at + b] = far_ref[b].astype(f32) - centre
         return 0
 
-    lax.fori_loop(0, blocks, prepare, 0)
+    lax.fori_loop(0, blocks // 4, prepare, 0)
+    first_valid = (index > 0).astype(f32)
+    last_valid = (index < segments).astype(f32)
+    taps_ref[0] = taps_in_ref[...] * first_valid
+    taps_ref[1] = taps_in_ref[...] * last_valid
     acc_ref[...] = jnp.zeros(acc_ref.shape, f32)
 
     def first(r, taper, dst):
@@ -232,34 +249,29 @@
 
     def both(taper, src, dst):
         def body(i, _):
-            second(i, src)
-            first(i, taper + 1, dst)
+            for j in range(UNROLL):
+                second(UNROLL * i + j, src)
+                first(UNROLL * i + j, taper, dst)
             return 0
 
-        lax.fori_loop(0, UNITS, body, 0)
+        lax.fori_loop(0, UNITS // UNROLL, body, 0)
 
     def start(i, _):
-        first(i, 0, ga_ref)
+        first(2 * i, 0, ga_ref)
+        first(2 * i + 1, 0, ga_ref)
         return 0
 
-    lax.fori_loop(0, chunks, start, 0)
+    lax.fori_loop(0, chunks // 2, start, 0)
 
     def pair(i, _):
-        both(2 * i, ga_ref, gb_ref)
-        both(2 * i + 1, gb_ref, ga_ref)
+        both(2 * i + 1, ga_ref, gb_ref)
+        both(jnp.minimum(2 * i + 2, tapers - 1), gb_ref, ga_ref)
         return 0
 
-    lax.fori_loop(0, tapers // 2 - 1, pair, 0)
-    both(tapers - 2, ga_ref, gb_ref)
-
-    def last(u, _):
-        second(u, gb_ref)
-        return 0
-
-    lax.fori_loop(0, UNITS, last, 0)
+    lax.fori_loop(0, tapers // 2, pair, 0)
 
     for u in range(UNITS):
-        t = (acc_ref[u].T * scale_ref[...]).astype(bf16)
+        t = (acc_ref[u].T * scale).astype(bf16)
         for d in range(groups):
             out_ref[d, u * rows_per : (u + 1) * rows_per, :] = t[d * rows_per : (d + 1) * rows_per]
 
@@ -275,6 +287,17 @@
         out_ref[i : i + 1, :] = sum_ref[r : r + 1, :]
 
 
+def merge_moments(mine, other, count):
+    gap = other[0:1] - mine[0:1]
+    row = lax.broadcasted_iota(jnp.int32, mine.shape, 0)
+    both = mine + other
+    return jnp.where(row == 0, both * 0.5, both + gap * gap * (count * 0.5))
+
+
+def params(mib):
+    return pltpu.CompilerParams(vmem_limit_bytes=mib * 2**20)
+
+
 def local(signal, tapers, eigenvalues):
     row_count, chan_count = signal.shape
     taper_count, seg = tapers.shape
@@ -282,20 +305,9 @@
     tm = lax.axis_size("tm")
     chans = lax.axis_size("chan")
     blocks = row_count // LANES
-    all_rows = row_count * tm
-    segments = all_rows // stride - 1
+    segments = row_count * tm // stride - 1
     half = chan_count // 2
     assert row_count == stride and half == LANES and seg == R * LANES
-    index = lax.axis_index("tm")
-    parity = index % 2
-
-    near = [(i, i ^ 1) for i in range(tm)]
-    far = [(i, i + 1 if i % 2 else i - 1) for i in range(1, tm - 1)]
-
-    keep = lax.dynamic_slice_in_dim(signal, parity * half, half, 1)
-    send = lax.dynamic_slice_in_dim(signal, (1 - parity) * half, half, 1)
-    near_raw = lax.ppermute(send, "tm", near)
-    far_raw = lax.ppermute(send, "tm", far)
 
     sums = jnp.sum(signal.astype(f32), axis=1).reshape(blocks, LANES)
     if chans == 2:
@@ -303,59 +315,61 @@
     else:
         total = lax.psum(sums, "chan")
     common = total / (chan_count * chans)
-    common_near = lax.ppermute(common, "tm", near)
-    common_far = lax.ppermute(common, "tm", far)
-
-    referenced, stats = pl.pallas_call(
+
+    block_shape = jax.ShapeDtypeStruct((blocks, LANES, LANES), bf16)
+    moments = jax.ShapeDtypeStruct((2, LANES), f32)
+    keep, send, stats, send_stats = pl.pallas_call(
         prep_kernel,
-        out_shape=(
-            jax.ShapeDtypeStruct((2, blocks, LANES, LANES), bf16),
-            jax.ShapeDtypeStruct((2, LANES), f32),
-        ),
+        out_shape=(block_shape, block_shape, moments, moments),
+        compiler_params=params(8),
         name="prep",
-    )(keep, near_raw, jnp.stack([common, common_near]))
-
-    mean, spread = stats[0], stats[1]
-    count = 2 * row_count
+    )(signal, common)
+
+    near_pairs = [(i, i ^ 1) for i in range(tm)]
+    far_pairs = [(i, i + 1 if i % 2 else i - 1) for i in range(1, tm - 1)]
+    other = lax.ppermute(send_stats, "tm", near_pairs)
+    near = lax.ppermute(send, "tm", near_pairs)
+    far = lax.ppermute(send, "tm", far_pairs)
+
+    count = row_count
+    stats = merge_moments(stats, other, count)
+    count *= 2
     step = 2
-    while step < tm:
-        other = lax.ppermute(jnp.stack([mean, spread]), "tm", [(i, i ^ step) for i in range(tm)])
-        gap = other[0] - mean
-        mean = (mean + other[0]) * 0.5
-        spread = spread + other[1] + gap * gap * (count * 0.5)
+    while tm // step > 4:
+        other = lax.ppermute(stats, "tm", [(i, i ^ step) for i in range(tm)])
+        stats = merge_moments(stats, other, count)
         count *= 2
         step *= 2
-    variance = spread / all_rows
-    scale = 1.0 / (segments * (variance + EPSILON))
+    parts = [stats] + [
+        lax.ppermute(stats, "tm", [(i, i ^ (step * k)) for i in range(tm)])
+        for k in range(1, tm // step)
+    ]
 
     weights = eigenvalues / jnp.sum(eigenvalues)
-    valid = jnp.stack([index > 0, index < tm - 1]).astype(f32)
-    taps = tapers.astype(f32) * jnp.sqrt(weights)[:, None]
-    taps = (valid[:, None, None] * taps[None]).reshape(2, taper_count, R, LANES)
-    order = jnp.stack([2 * (1 - parity), 2 * parity]).astype(jnp.int32)
+    taps = (tapers.astype(f32) * jnp.sqrt(weights)[:, None]).reshape(taper_count, R, LANES)
     table = jnp.asarray(unit_tables(seg, tm))
 
-    vmem = pl.BlockSpec(memory_space=pltpu.VMEM)
-    parts = pl.pallas_call(
-        main_kernel,
+    partial = pl.pallas_call(
+        functools.partial(main_kernel, segments, count),
         out_shape=jax.ShapeDtypeStruct((tm, stride // tm, LANES), bf16),
-        in_specs=[pl.BlockSpec(memory_space=pltpu.SMEM)] + [vmem] * 7,
-        out_specs=vmem,
         scratch_shapes=[
+            pltpu.VMEM((2, taper_count, R, LANES), f32),
             pltpu.VMEM((3 * blocks, LANES, LANES), f32),
             pltpu.VMEM((UNITS, 2 * LANES, 2 * LANES), bf16),
             pltpu.VMEM((UNITS, 2 * LANES, 2 * LANES), bf16),
             pltpu.VMEM((UNITS, LANES, LANES), f32),
         ],
+        compiler_params=params(24),
         name="spectra",
-    )(order, referenced, far_raw, common_far, mean[None], scale[None], taps, table)
-
-    got = lax.all_to_all(parts, "tm", 0, 0, tiled=True)
+    )(keep, near, far, *parts, taps, table)
+
+    got = lax.all_to_all(partial, "tm", 0, 0, tiled=True)
     rows = bin_rows(tm, seg)
     return pl.pallas_call(
-        lambda *refs: merge_kernel(rows, *refs),
+        functools.partial(merge_kernel, rows),
         out_shape=jax.ShapeDtypeStruct((stride // tm, chan_count), f32),
         scratch_shapes=[pltpu.VMEM((stride // tm, chan_count), f32)],
+        compiler_params=params(4),
         name="merge",
     )(got)
 

time: 89 us -> 68 us (0.76)
  Pallas kernels: 39.5 us -> 19.3 us
  waiting for transfers between devices: 4.21 us -> 8.7 us
  starting transfers between devices: 14.4 us -> 11.7 us
  other arithmetic: 5.07 us -> 3.1 us
  local copies, waits for them, and re-layouts: 3.83 us -> 2.85 us
    pallas_call x3, Pallas kernels: 39.5 us -> 19.3 us  [the longest x1 17.3 us: local(): pl.pallas_call(functools.partial(main_kernel, segments, count), out_shape...]
    ppermute x7, starting transfers between devices: 11.8 us -> 8.66 us  [the longest x3 5.77 us: local(): lax.ppermute(stats, 'tm', [(i, i ^ step * k) for i in range(tm)])]
    ppermute x7, waiting for transfers between devices: 3.94 us -> 7.07 us  [the longest x3 6.43 us: local(): lax.ppermute(stats, 'tm', [(i, i ^ step * k) for i in range(tm)])]
    dynamic_slice x1 -> x0, local copies, waits for them, and re-layouts: 2.19 us -> none  [local(): send = lax.dynamic_slice_in_dim(signal, (1 - parity) * half, half, 1)]
    ppermute x1, waiting for transfers between devices: 0.27 us -> 1.63 us  [local(): total = sums + lax.ppermute(sums, 'chan', [(0, 1), (1, 0)])]
    reduce_sum x1, other arithmetic: 0.34 us -> 1.6 us  [local(): sums = jnp.sum(signal.astype(f32), axis=1).reshape(blocks, LANES)]
    unnamed x12 -> x9, local copies, waits for them, and re-layouts: 1.61 us -> 2.85 us
    another operation x5 -> x0, other arithmetic: 1.21 us -> none  [the longest x2 0.61 us: local(): jnp.stack([common, common_near])]
  transfers between devices with their start and end apart: 8 -> 8, of which waited for: 5 -> 6; matrix products, arithmetic and copies ran while one was open for 6% -> 2% of each run, Pallas kernels for 5% -> 0%
where the time goes in v2:
time: 68 us; the launch traced here: 67.7 us
  blocking collectives  22 us (32%)
  Pallas kernels  19.3 us (28%)
  starting transfers between devices  11.7 us (17%)
  waiting for transfers between devices  8.7 us (13%)
  other arithmetic  3.1 us (5%)
  local copies, waits for them, and re-layouts  2.85 us (4%)
    all_to_all x1, blocking collectives, local(): got = lax.all_to_all(partial, 'tm', 0, 0, tiled=True)  22 us
    pallas_call x1, Pallas kernels, local(): pl.pallas_call(functools.partial(main_kernel, segments, count), out_shape...  17.3 us
    ppermute x3, waiting for transfers between devices, local(): lax.ppermute(stats, 'tm', [(i, i ^ step * k) for i in range(tm)])  6.43 us
    ppermute x3, starting transfers between devices, local(): lax.ppermute(stats, 'tm', [(i, i ^ step * k) for i in range(tm)])  5.77 us
    ppermute x1, starting transfers between devices, local(): total = sums + lax.ppermute(sums, 'chan', [(0, 1), (1, 0)])  3.03 us
    unnamed x9, local copies, waits for them, and re-layouts  2.85 us
    ppermute x1, starting transfers between devices, local(): other = lax.ppermute(stats, 'tm', [(i, i ^ step) for i in range(tm)])  2.05 us
    ppermute x1, waiting for transfers between devices, local(): total = sums + lax.ppermute(sums, 'chan', [(0, 1), (1, 0)])  1.63 us
  transfers between devices with their start and end apart: 8, of which 6 were waited for; matrix products, arithmetic and copies ran while one was open for 2% of the time, Pallas kernels for 0%

profile of v2, /device:TPU:0, one launch (start us, length us, event | category | flops | bytes accessed | tf_op | source)
XLA Modules:
  0.0 67.7 jit_solution(9317516861709362701)
XLA Ops:
  0.0 0.0 copy-start.3
  0.0 0.0 copy-start.2
  0.0 1.6 %convert_reduce_fusion = f32[2048]{0:T(1024)S(1)} fusion(bf16[2048,256]{1,0:T(8,128)(2,1)} %signal_ref.1), kind=kLoop, calls=%fused_computation | loop fusion | flops 1046528 | bytes 1056768 | tf_op jit(solution)/shard_map/reduce_sum | solution.py:312
  1.6 3.0 %collective-permute-start = (f32[16,128]{1,0:T(8,128)S(1)}, f32[16,128]{1,0:T(8,128)S(1)}, u32[]{:S(2)}, u32[]{:S(2)}) collective-permute-start(f32[16,128]{1,0:T(8,128)S(1)} %bitcast.12), channel_id=1, source_target_pairs={{0,1},{1,0},{2,3},{3,2},{4,5},{5,4},{6,7},{7,6},{8,9},{9,8},{10,11... | collective-permute-start | bytes 24584 | tf_op jit(solution)/shard_map/ppermute | solution.py:314
  4.6 1.6 %collective-permute-done = f32[16,128]{1,0:T(8,128)S(1)} collective-permute-done((f32[16,128]{1,0:T(8,128)S(1)}, f32[16,128]{1,0:T(8,128)S(1)}, u32[]{:S(2)}, u32[]{:S(2)}) %collective-permute-start) | collective-permute-done | bytes 8224 | tf_op jit(solution)/shard_map/ppermute | solution.py:314
  6.3 1.2 %copy-done = bf16[2048,256]{1,0:T(8,128)(2,1)S(1)} copy-done((bf16[2048,256]{1,0:T(8,128)(2,1)S(1)}, bf16[2048,256]{1,0:T(8,128)(2,1)}, u32[]{:S(2)}) %copy-start) | copy-done | bytes 1048600
  7.5 1.2 %prep.1 = (bf16[16,128,128]{2,1,0:T(8,128)(2,1)S(1)}, bf16[16,128,128]{2,1,0:T(8,128)(2,1)S(1)}, f32[2,128]{1,0:T(2,128)S(1)}, f32[2,128]{1,0:T(2,128)S(1)}) custom-call(bf16[2048,256]{1,0:T(8,128)(2,1)S(1)} %copy-done, f32[16,128]{1,0:T(8,128)S(1)} %add_multiply_fusion.common_ref), custom_call_target="tpu_custom_call" | custom-call | tf_op jit(solution)/shard_map/prep/pallas_call | solution.py:321
  8.7 0.1 collective-permute-start.3
  8.8 0.0 copy-done.3
  8.8 0.6 reduce_sum.19
  9.4 0.5 collective-permute-done.3
  10.0 0.1 add_select_fusion.1
  10.0 2.0 %collective-permute-start.4 = (f32[2,128]{1,0:T(2,128)S(1)}, f32[2,128]{1,0:T(2,128)S(1)}, u32[]{:S(2)}, u32[]{:S(2)}) collective-permute-start(f32[2,128]{1,0:T(2,128)S(1)} %add_select_fusion.1), channel_id=1, source_target_pairs={{0,4},{2,6},{4,0},{6,2},{8,12},{10,14},{12,8},{14,10},{16,20},{18,... | collective-permute-start | bytes 3080 | tf_op jit(solution)/shard_map/ppermute | solution.py:339
  12.1 0.7 divide_sqrt_fusion
  12.7 0.1 collective-permute-start.1
  12.8 0.7 %collective-permute-start.2 = (bf16[16,128,128]{2,1,0:T(8,128)(2,1)S(1)}, bf16[16,128,128]{2,1,0:T(8,128)(2,1)S(1)}, u32[]{:S(2)}, u32[]{:S(2)}) collective-permute-start(bf16[16,128,128]{2,1,0:T(8,128)(2,1)S(1)} %get-tuple-element.10), channel_id=1, source_target_pairs={{2,4},{4,2},{6,8},{8,6},{10,12},{12,10},{14,16},{16,14},{18,20},{2... | collective-permute-start | bytes 1572872 | tf_op jit(solution)/shard_map/ppermute | solution.py:332
  13.5 0.1 collective-permute-done.4
  13.6 0.1 add_select_fusion.refs_0_
  13.7 2.7 %collective-permute-start.5 = (f32[2,128]{1,0:T(2,128)S(1)}, f32[2,128]{1,0:T(2,128)S(1)}, u32[]{:S(2)}, u32[]{:S(2)}) collective-permute-start(f32[2,128]{1,0:T(2,128)S(1)} %add_select_fusion.refs_0_), channel_id=1, source_target_pairs={{0,8},{2,10},{4,12},{6,14},{8,0},{10,2},{12,4},{14,6},{16,24},{18,... | collective-permute-start | bytes 3080 | tf_op jit(solution)/shard_map/ppermute | solution.py:344
  16.4 3.1 %collective-permute-start.6 = (f32[2,128]{1,0:T(2,128)S(1)}, f32[2,128]{1,0:T(2,128)S(1)}, u32[]{:S(2)}, u32[]{:S(2)}) collective-permute-start(f32[2,128]{1,0:T(2,128)S(1)} %add_select_fusion.refs_0_), channel_id=1, source_target_pairs={{0,16},{2,18},{4,20},{6,22},{8,24},{10,26},{12,28},{14,30},{16,0},... | collective-permute-start | bytes 3080 | tf_op jit(solution)/shard_map/ppermute | solution.py:344
  19.5 0.0 collective-permute-start.7
  19.5 0.0 copy-done.2
  19.5 0.1 multiply_bitcast_fusion
  19.6 3.9 %collective-permute-done.5.refs_1_ = f32[2,128]{1,0:T(2,128)S(1)} collective-permute-done((f32[2,128]{1,0:T(2,128)S(1)}, f32[2,128]{1,0:T(2,128)S(1)}, u32[]{:S(2)}, u32[]{:S(2)}) %collective-permute-start.5) | collective-permute-done | bytes 1056 | tf_op jit(solution)/shard_map/ppermute | solution.py:344
  23.5 1.5 %collective-permute-done.6.refs_2_ = f32[2,128]{1,0:T(2,128)S(1)} collective-permute-done((f32[2,128]{1,0:T(2,128)S(1)}, f32[2,128]{1,0:T(2,128)S(1)}, u32[]{:S(2)}, u32[]{:S(2)}) %collective-permute-start.6) | collective-permute-done | bytes 1056 | tf_op jit(solution)/shard_map/ppermute | solution.py:344
  25.0 1.0 %collective-permute-done.7.refs_3_ = f32[2,128]{1,0:T(2,128)S(1)} collective-permute-done((f32[2,128]{1,0:T(2,128)S(1)}, f32[2,128]{1,0:T(2,128)S(1)}, u32[]{:S(2)}, u32[]{:S(2)}) %collective-permute-start.7) | collective-permute-done | bytes 1056 | tf_op jit(solution)/shard_map/ppermute | solution.py:344
  26.0 0.0 collective-permute-done.1.near_ref
  26.0 0.0 collective-permute-done.2.far_ref
  26.0 1.6 %copy-done.1 = bf16[16,256,256]{2,1,0:T(8,128)(2,1)S(1)} copy-done((bf16[16,256,256]{2,1,0:T(8,128)(2,1)S(1)}, bf16[16,256,256]{2,1,0:T(8,128)(2,1)}, u32[]{:S(2)}) %copy-start.1) | copy-done | bytes 2097176
  27.6 17.3 %spectra.1 = bf16[16,128,128]{2,1,0:T(8,128)(2,1)S(1)} custom-call(bf16[16,128,128]{2,1,0:T(8,128)(2,1)S(1)} %get-tuple-element.9.keep_ref, bf16[16,128,128]{2,1,0:T(8,128)(2,1)S(1)} %collective-permute-done.1.near_ref, bf16[16,128,128]{2,1,0:T(8,128)(2,1)S(1)} %collective-permute-done.2.far_ref, f32[2,128]{1,0:T(2,128)S(1)} %add_select_fusion.refs_0_, ...), custom_call_target="tpu_custom_call" | custom-call | tf_op jit(solution)/shard_map/spectra/pallas_call | solution.py:352
  44.9 22.0 %all_to_all.5.parts_ref = bf16[16,128,128]{2,1,0:T(8,128)(2,1)S(1)} all-to-all(bf16[16,128,128]{2,1,0:T(8,128)(2,1)S(1)} %spectra.1), channel_id=1, replica_groups=mesh['tm'=16,'chan'=2] {'tm'}, dimensions={0} | all-to-all | bytes 1048576 | tf_op jit(solution)/shard_map/all_to_all | solution.py:366
  66.9 0.8 %merge.1 = f32[128,256]{1,0:T(8,128)} custom-call(bf16[16,128,128]{2,1,0:T(8,128)(2,1)S(1)} %all_to_all.5.parts_ref), custom_call_target="tpu_custom_call" | custom-call | tf_op jit(solution)/shard_map/merge/pallas_call | solution.py:368
  (7 shorter events, 0.1 us)
Async XLA Ops:
  0.0 8.8 %copy-start.3 = (f32[8]{0:T(128)S(1)}, f32[8]{0:T(128)}, u32[]{:S(2)}) copy-start(f32[8]{0:T(128)} %param.6) | copy-start | bytes 100
  0.0 19.5 %copy-start.2 = (bf16[8,4096]{1,0:T(8,128)(2,1)S(1)}, bf16[8,4096]{1,0:T(8,128)(2,1)}, u32[]{:S(2)}) copy-start(bf16[8,4096]{1,0:T(8,128)(2,1)} %param.5) | copy-start | bytes 196612
  1.6 4.7 %collective-permute-start = (f32[16,128]{1,0:T(8,128)S(1)}, f32[16,128]{1,0:T(8,128)S(1)}, u32[]{:S(2)}, u32[]{:S(2)}) collective-permute-start(f32[16,128]{1,0:T(8,128)S(1)} %bitcast.12), channel_id=1, source_target_pairs={{0,1},{1,0},{2,3},{3,2},{4,5},{5,4},{6,7},{7,6},{8,9},{9,8},{10,11... | collective-permute-start | bytes 24584 | tf_op jit(solution)/shard_map/ppermute | solution.py:314
  6.3 1.2 %copy-start = (bf16[2048,256]{1,0:T(8,128)(2,1)S(1)}, bf16[2048,256]{1,0:T(8,128)(2,1)}, u32[]{:S(2)}) copy-start(bf16[2048,256]{1,0:T(8,128)(2,1)} %signal_ref.1) | copy-start | bytes 3145732
  8.7 1.2 %collective-permute-start.3 = (f32[2,128]{1,0:T(2,128)S(1)}, f32[2,128]{1,0:T(2,128)S(1)}, u32[]{:S(2)}, u32[]{:S(2)}) collective-permute-start(f32[2,128]{1,0:T(2,128)S(1)} %get-tuple-element.12), channel_id=1, source_target_pairs={{0,2},{2,0},{4,6},{6,4},{8,10},{10,8},{12,14},{14,12},{16,18},{18,... | collective-permute-start | bytes 3080 | tf_op jit(solution)/shard_map/ppermute | solution.py:330
  10.0 3.6 %collective-permute-start.4 = (f32[2,128]{1,0:T(2,128)S(1)}, f32[2,128]{1,0:T(2,128)S(1)}, u32[]{:S(2)}, u32[]{:S(2)}) collective-permute-start(f32[2,128]{1,0:T(2,128)S(1)} %add_select_fusion.1), channel_id=1, source_target_pairs={{0,4},{2,6},{4,0},{6,2},{8,12},{10,14},{12,8},{14,10},{16,20},{18,... | collective-permute-start | bytes 3080 | tf_op jit(solution)/shard_map/ppermute | solution.py:339
  12.7 13.3 %collective-permute-start.1 = (bf16[16,128,128]{2,1,0:T(8,128)(2,1)S(1)}, bf16[16,128,128]{2,1,0:T(8,128)(2,1)S(1)}, u32[]{:S(2)}, u32[]{:S(2)}) collective-permute-start(bf16[16,128,128]{2,1,0:T(8,128)(2,1)S(1)} %get-tuple-element.10), channel_id=1, source_target_pairs={{0,2},{2,0},{4,6},{6,4},{8,10},{10,8},{12,14},{14,12},{16,18},{18,... | collective-permute-start | bytes 1572872 | tf_op jit(solution)/shard_map/ppermute | solution.py:331
  12.8 13.2 %collective-permute-start.2 = (bf16[16,128,128]{2,1,0:T(8,128)(2,1)S(1)}, bf16[16,128,128]{2,1,0:T(8,128)(2,1)S(1)}, u32[]{:S(2)}, u32[]{:S(2)}) collective-permute-start(bf16[16,128,128]{2,1,0:T(8,128)(2,1)S(1)} %get-tuple-element.10), channel_id=1, source_target_pairs={{2,4},{4,2},{6,8},{8,6},{10,12},{12,10},{14,16},{16,14},{18,20},{2... | collective-permute-start | bytes 1572872 | tf_op jit(solution)/shard_map/ppermute | solution.py:332
  13.7 9.8 %collective-permute-start.5 = (f32[2,128]{1,0:T(2,128)S(1)}, f32[2,128]{1,0:T(2,128)S(1)}, u32[]{:S(2)}, u32[]{:S(2)}) collective-permute-start(f32[2,128]{1,0:T(2,128)S(1)} %add_select_fusion.refs_0_), channel_id=1, source_target_pairs={{0,8},{2,10},{4,12},{6,14},{8,0},{10,2},{12,4},{14,6},{16,24},{18,... | collective-permute-start | bytes 3080 | tf_op jit(solution)/shard_map/ppermute | solution.py:344
  16.4 8.6 %collective-permute-start.6 = (f32[2,128]{1,0:T(2,128)S(1)}, f32[2,128]{1,0:T(2,128)S(1)}, u32[]{:S(2)}, u32[]{:S(2)}) collective-permute-start(f32[2,128]{1,0:T(2,128)S(1)} %add_select_fusion.refs_0_), channel_id=1, source_target_pairs={{0,16},{2,18},{4,20},{6,22},{8,24},{10,26},{12,28},{14,30},{16,0},... | collective-permute-start | bytes 3080 | tf_op jit(solution)/shard_map/ppermute | solution.py:344
  19.5 6.6 %collective-permute-start.7 = (f32[2,128]{1,0:T(2,128)S(1)}, f32[2,128]{1,0:T(2,128)S(1)}, u32[]{:S(2)}, u32[]{:S(2)}) collective-permute-start(f32[2,128]{1,0:T(2,128)S(1)} %add_select_fusion.refs_0_), channel_id=1, source_target_pairs={{0,24},{2,26},{4,28},{6,30},{8,16},{10,18},{12,20},{14,22},{16,8},... | collective-permute-start | bytes 3080 | tf_op jit(solution)/shard_map/ppermute | solution.py:344
  26.0 1.6 %copy-start.1 = (bf16[16,256,256]{2,1,0:T(8,128)(2,1)S(1)}, bf16[16,256,256]{2,1,0:T(8,128)(2,1)}, u32[]{:S(2)}) copy-start(bf16[16,256,256]{2,1,0:T(8,128)(2,1)} %constant.15.clone.refs_5_) | copy-start | bytes 6291460
